TPU v7x, 32 devices: a whole 2x2x4 slice. The times are simulated.
32 devices in a mesh: zero: 16 (over z, x, core), tensor: 2 (over y).
Axes of the slice: x: 2, y: 2, z: 4, core: 2. Of those that a mesh axis runs over, the one named last changes fastest.
Arguments:
- grads: bfloat16 [16, 2, 16, 49152], P('zero', None, None, 'tensor'), may hold values from -1200 to 1200
- moment1: bfloat16 [2, 16, 49152], P(None, 'zero', 'tensor'), may hold values from -1 to 1
- moment2: float32 [2, 16, 49152], P(None, 'zero', 'tensor'), may hold values from 0.01 to 0.2
- master: float32 [2, 16, 49152], P(None, 'zero', 'tensor'), may hold values from -0.008 to 0.008
Outputs:
- new_moment1: bfloat16 [2, 16, 49152], P(None, 'zero', 'tensor')
- new_moment2: float32 [2, 16, 49152], P(None, 'zero', 'tensor')
- new_master: float32 [2, 16, 49152], P(None, 'zero', 'tensor')
- weights: bfloat16 [2, 16, 49152], P(None, None, 'tensor')
All inputs are finite; a program needn't handle non-finite values. Where the computation divides by a largest or mean magnitude, that divisor is 1e-20 or more.
Results may differ from a plain program's by a relative error of at most 0.0053.
Values may be sent and summed in bfloat16 or wider, within the bound.
A program may use at most 64 MiB of HBM per device.

v0:
```python
import jax
import jax.numpy as jnp
from jax import lax
from jax.sharding import PartitionSpec as P

decay_first = 0.9
decay_second = 0.95
learn_rate = 0.001
weight_decay = 0.1
adam_epsilon = 1e-08
peak_epsilon = 1e-06
bias_first = 1.0 - 0.9**10
bias_second = 1.0 - 0.95**10


def update_rows(gsum, moment1, moment2, master):
    new_moment1 = (decay_first * moment1.astype(jnp.float32) + (1.0 - decay_first) * gsum).astype(
        jnp.bfloat16
    )
    new_moment2 = decay_second * moment2 + (1.0 - decay_second) * gsum * gsum
    stored = lax.optimization_barrier(new_moment1).astype(jnp.float32)
    step_dir = stored / bias_first / (jnp.sqrt(new_moment2 / bias_second) + adam_epsilon)
    new_master = master - learn_rate * (step_dir + weight_decay * master)
    local_peak = jnp.max(jnp.abs(new_master), axis=(1, 2))
    wpeak = lax.pmax(local_peak, ("zero", "tensor")) + peak_epsilon
    normed = (new_master / wpeak[:, None, None]).astype(jnp.bfloat16)
    weights = lax.all_gather(normed, "zero", axis=1, tiled=True)
    return (new_moment1, new_moment2, new_master, weights)


def local(grads, moment1, moment2, master):
    local_peak = jnp.max(jnp.abs(grads), axis=(0, 2, 3)).astype(jnp.float32)
    peak = lax.pmax(local_peak, ("zero", "tensor")) + peak_epsilon
    scaled_half = (grads.astype(jnp.float32) / peak[None, :, None, None]).astype(jnp.bfloat16)
    received = lax.all_to_all(scaled_half, "zero", split_axis=2, concat_axis=0, tiled=True)
    gsum = jnp.sum(received.astype(jnp.float32), axis=0)
    return update_rows(gsum, moment1, moment2, master)


def solution(mesh):
    placed = (
        P("zero", None, None, "tensor"),
        P(None, "zero", "tensor"),
        P(None, "zero", "tensor"),
        P(None, "zero", "tensor"),
    )
    return jax.shard_map(
        local,
        mesh=mesh,
        in_specs=placed,
        out_specs=(
            P(None, "zero", "tensor"),
            P(None, "zero", "tensor"),
            P(None, "zero", "tensor"),
            P(None, None, "tensor"),
        ),
        check_vma=False,
    )
```

profile of v0, /device:TPU:0, one launch (start us, length us, event | category | flops | bytes accessed | tf_op | source)
XLA Modules:
  0.0 187.2 jit_solution(13088254821506365265)
XLA Ops:
  7.2 0.0 copy-start
  7.2 0.0 all-gather.2.cloned.1.call-start
  7.2 1.8 abs_reduce_fusion
  9.0 42.0 %pmax.14 = f32[2]{0:T(128)S(1)} all-reduce(bf16[2]{0:T(256)(128)(2,1)S(1)} %abs_reduce_fusion), channel_id=1, replica_groups=mesh['zero'=16,'tensor'=2] {'zero','tensor'}, use_global_device_ids=true, to_apply=%region_1.0 | all-reduce | flops 2 | bytes 12 | tf_op jit(solution)/shard_map/pmax | solution.py:33
  51.0 0.0 copy-done
  51.0 0.3 divide_convert_fusion
  51.3 1.6 copy.17
  52.9 41.1 %all_to_all.4 = bf16[1,2,16,24576]{3,1,0,2:T(2,128)(2,1)S(1)} all-to-all(bf16[1,2,16,24576]{3,1,0,2:T(2,128)(2,1)S(1)} %copy.17), channel_id=1, replica_groups=mesh['zero'=16,'tensor'=2] {'zero'}, dimensions={2} | all-to-all | bytes 3145728 | tf_op jit(solution)/shard_map/all_to_all | solution.py:35
  94.1 0.0 copy-start.4
  94.1 1.4 convert_reduce_fusion
  95.4 0.0 copy-done.4
  95.4 0.2 fusion.2
  95.6 0.0 copy-done.2
  95.6 0.0 copy-done.3
  95.6 0.0 copy-start.1
  95.6 0.8 abs_reduce_fusion.1
  96.5 40.1 %pmax.15 = f32[2]{0:T(128)S(1)} all-reduce(f32[2]{0:T(128)S(1)} %get-tuple-element.16), channel_id=1, replica_groups=mesh['zero'=16,'tensor'=2] {'zero','tensor'}, use_global_device_ids=true, to_apply=%region_4.0 | all-reduce | flops 2 | bytes 16 | tf_op jit(solution)/shard_map/pmax | solution.py:25
  136.6 0.8 divide_convert_fusion.1
  137.4 0.0 all-gather.2.cloned.1.call-update
  137.4 0.9 copy.22
  138.3 0.9 copy.21
  139.2 37.7 %all-gather.2.cloned.1.call-done = bf16[2,16,24576]{2,0,1:T(2,128)(2,1)} async-done(((bf16[2,1,24576]{2,0,1:T(2,128)(2,1)}), bf16[2,16,24576]{2,0,1:T(2,128)(2,1)}) %all-gather.2.cloned.1.call-update) | async-done | bytes 1572880 | tf_op jit(solution)/shard_map/all_gather | solution.py:27
  176.9 3.4 %copy.23 = bf16[2,16,24576]{2,1,0:T(8,128)(2,1)} copy(bf16[2,16,24576]{2,0,1:T(2,128)(2,1)} %all-gather.2.cloned.1.call-done) | data formatting | bytes 3145728
  180.3 0.0 copy-done.1
  (4 shorter events, 0.0 us)
Async XLA Ops:
  7.2 43.8 %copy-start = (bf16[1,2,16,24576]{3,2,1,0:T(8,128)(2,1)S(1)}, bf16[1,2,16,24576]{3,2,1,0:T(8,128)(2,1)}, u32[]{:S(2)}) copy-start(bf16[1,2,16,24576]{3,2,1,0:T(8,128)(2,1)} %param.4) | copy-start | bytes 4718596
  7.2 169.7 %all-gather.2.cloned.1.call-start = ((), (), s32[]{:S(2)}) async-start(), calls=%async_computation.1 | async-start | bytes 1671168 | tf_op jit(solution)/shard_map/all_gather | solution.py:27
  94.1 1.4 copy-start.4
  94.1 1.6 copy-start.2
  94.1 1.6 copy-start.3
  95.6 84.7 %copy-start.1 = (bf16[2,1,24576]{2,0,1:T(2,128)(2,1)}, bf16[2,1,24576]{2,0,1:T(2,128)(2,1)S(1)}, u32[]{:S(2)}) copy-start(bf16[2,1,24576]{2,0,1:T(2,128)(2,1)S(1)} %fusion.2) | copy-start | bytes 294916
Sparse Core Ops, SparseCore 0:
  137.5 39.3 all-gather.1
where the time goes:
time: 188 us; the launch traced here: 187 us
  blocking collectives  123 us (65%)
  waiting for transfers between devices  37.8 us (20%)
  between operations  14.1 us (8%)
  local copies, waits for them, and re-layouts  6.81 us (4%)
  other arithmetic  5.24 us (3%)
    pmax x1, blocking collectives, local(): peak = lax.pmax(local_peak, ('zero', 'tensor')) + peak_epsilon  42 us
    all_to_all x1, blocking collectives, local(): lax.all_to_all(scaled_half, 'zero', split_axis=2, concat_axis=0, tiled=True)  41.1 us
    pmax x1, blocking collectives, update_rows(): wpeak = lax.pmax(local_peak, ('zero', 'tensor')) + peak_epsilon  40.1 us
    all_gather x1, waiting for transfers between devices, update_rows(): weights = lax.all_gather(normed, 'zero', axis=1, tiled=True)  37.7 us
    unnamed x13, local copies, waits for them, and re-layouts  5.2 us
  transfers between devices with their start and end apart: 1, of which 1 were waited for; matrix products, arithmetic and copies ran while one was open for 1% of the time, Pallas kernels for 0%

commit v1 on v0

--- a/solution.py
+++ b/solution.py
@@ -13,6 +13,25 @@
 bias_second = 1.0 - 0.95**10
 
 
+def ring_gather(value, axis, dim):
+    size, here, span = (lax.axis_size(axis), lax.axis_index(axis), value.shape[dim])
+    right = [(i, (i + 1) % size) for i in range(size)]
+    downward = [(i, (i - 1) % size) for i in range(size)]
+    out = jnp.zeros((*value.shape[:dim], size * span, *value.shape[dim + 1 :]), value.dtype)
+    out = lax.dynamic_update_slice_in_dim(out, value, here * span, axis=dim)
+    from_left = from_right = value
+    half = size // 2
+    for hop in range(1, half + 1):
+        from_left = lax.ppermute(from_left, axis, right)
+        out = lax.dynamic_update_slice_in_dim(out, from_left, (here - hop) % size * span, axis=dim)
+        if hop < size - half:
+            from_right = lax.ppermute(from_right, axis, downward)
+            out = lax.dynamic_update_slice_in_dim(
+                out, from_right, (here + hop) % size * span, axis=dim
+            )
+    return out
+
+
 def update_rows(gsum, moment1, moment2, master):
     new_moment1 = (decay_first * moment1.astype(jnp.float32) + (1.0 - decay_first) * gsum).astype(
         jnp.bfloat16
@@ -24,7 +43,7 @@
     local_peak = jnp.max(jnp.abs(new_master), axis=(1, 2))
     wpeak = lax.pmax(local_peak, ("zero", "tensor")) + peak_epsilon
     normed = (new_master / wpeak[:, None, None]).astype(jnp.bfloat16)
-    weights = lax.all_gather(normed, "zero", axis=1, tiled=True)
+    weights = ring_gather(normed, "zero", 1)
     return (new_moment1, new_moment2, new_master, weights)
 
 

time: 188 us -> 238 us (1.27)
  local copies, waits for them, and re-layouts: 6.81 us -> 60.9 us
  starting transfers between devices: 0.04 us -> 31.7 us
  waiting for transfers between devices: 37.8 us -> 15.7 us
  between operations: 14.1 us -> 1.01 us
    dynamic_update_slice x0 -> x16, local copies, waits for them, and re-layouts: none -> 53.8 us  [the longest x8 26.9 us: ring_gather(): lax.dynamic_update_slice_in_dim(out, from_left, (here - hop) % size * spa...]
    all_gather x1 -> x0, waiting for transfers between devices: 37.7 us -> none  [update_rows(): weights = lax.all_gather(normed, 'zero', axis=1, tiled=True)]
    ppermute x0 -> x15, starting transfers between devices: none -> 31.7 us  [the longest x7 31.6 us: ring_gather(): from_right = lax.ppermute(from_right, axis, downward)]
    ppermute x0 -> x15, waiting for transfers between devices: none -> 15.7 us  [the longest x8 15.6 us: ring_gather(): from_left = lax.ppermute(from_left, axis, right)]
    unnamed x13 -> x14, local copies, waits for them, and re-layouts: 5.2 us -> 2.92 us
  transfers between devices with their start and end apart: 1 -> 15, of which waited for: 1 -> 8; matrix products, arithmetic and copies ran while one was open for 1% -> 23% of each run, Pallas kernels for 0% -> 0%
where the time goes in v1:
time: 238 us; the launch traced here: 237 us
  blocking collectives  123 us (52%)
  local copies, waits for them, and re-layouts  60.9 us (26%)
  starting transfers between devices  31.7 us (13%)
  waiting for transfers between devices  15.7 us (7%)
  other arithmetic  4.61 us (2%)
    pmax x1, blocking collectives, local(): peak = lax.pmax(local_peak, ('zero', 'tensor')) + peak_epsilon  42 us
    all_to_all x1, blocking collectives, local(): lax.all_to_all(scaled_half, 'zero', split_axis=2, concat_axis=0, tiled=True)  41.1 us
    pmax x1, blocking collectives, update_rows(): wpeak = lax.pmax(local_peak, ('zero', 'tensor')) + peak_epsilon  40.1 us
    ppermute x7, starting transfers between devices, ring_gather(): from_right = lax.ppermute(from_right, axis, downward)  31.6 us
    dynamic_update_slice x8, local copies, waits for them, and re-layouts, ring_gather(): lax.dynamic_update_slice_in_dim(out, from_left, (here - hop) % size * spa...  26.9 us
    dynamic_update_slice x7, local copies, waits for them, and re-layouts, ring_gather(): lax.dynamic_update_slice_in_dim(out, from_right, (here + hop) % size * sp...  23.5 us
    ppermute x8, waiting for transfers between devices, ring_gather(): from_left = lax.ppermute(from_left, axis, right)  15.6 us
  transfers between devices with their start and end apart: 15, of which 8 were waited for; matrix products, arithmetic and copies ran while one was open for 23% of the time, Pallas kernels for 0%

profile of v1, /device:TPU:0, one launch (start us, length us, event | category | flops | bytes accessed | tf_op | source)
XLA Modules:
  0.0 237.1 jit_solution(6466603162862122773)
XLA Ops:
  2.4 42.0 %pmax.14 = f32[2]{0:T(128)S(1)} all-reduce(bf16[2]{0:T(256)(128)(2,1)S(1)} %abs_reduce_fusion), channel_id=1, replica_groups=mesh['zero'=16,'tensor'=2] {'zero','tensor'}, use_global_device_ids=true, to_apply=%region_1.0 | all-reduce | flops 2 | bytes 12 | tf_op jit(solution)/shard_map/pmax | solution.py:52
  46.3 41.1 %all_to_all.4 = bf16[1,2,16,24576]{3,1,0,2:T(2,128)(2,1)S(1)} all-to-all(bf16[1,2,16,24576]{3,1,0,2:T(2,128)(2,1)S(1)} %copy.32), channel_id=1, replica_groups=mesh['zero'=16,'tensor'=2] {'zero'}, dimensions={2} | all-to-all | bytes 3145728 | tf_op jit(solution)/shard_map/all_to_all | solution.py:54
  89.9 40.1 %pmax.15 = f32[2]{0:T(128)S(1)} all-reduce(f32[2]{0:T(128)S(1)} %get-tuple-element.16), channel_id=1, replica_groups=mesh['zero'=16,'tensor'=2] {'zero','tensor'}, use_global_device_ids=true, to_apply=%region_4.0 | all-reduce | flops 2 | bytes 16 | tf_op jit(solution)/shard_map/pmax | solution.py:44
  130.2 4.4 %collective-permute-start.1 = (bf16[2,1,24576]{2,0,1:T(2,128)(2,1)S(1)}, bf16[2,1,24576]{2,0,1:T(2,128)(2,1)S(1)}, u32[]{:S(2)}, u32[]{:S(2)}) collective-permute-start(bf16[2,1,24576]{2,0,1:T(2,128)(2,1)S(1)} %divide_convert_fusion.1), channel_id=1, source_target_pairs={{0,30},{2,0},{4,2},{6,4},{8,6},{10,8},{12,10},{14,12},{16,14},{18,... | collective-permute-start | bytes 294920 | tf_op jit(solution)/shard_map/ppermute | solution.py:28
  137.0 4.4 %collective-permute-start.3 = (bf16[2,1,24576]{2,0,1:T(2,128)(2,1)S(1)}, bf16[2,1,24576]{2,0,1:T(2,128)(2,1)S(1)}, u32[]{:S(2)}, u32[]{:S(2)}) collective-permute-start(bf16[2,1,24576]{2,0,1:T(2,128)(2,1)S(1)} %collective-permute-done.1), channel_id=1, source_target_pairs={{0,30},{2,0},{4,2},{6,4},{8,6},{10,8},{12,10},{14,12},{16,14},{18,... | collective-permute-start | bytes 294920 | tf_op jit(solution)/shard_map/ppermute | solution.py:28
  143.8 4.4 %collective-permute-start.5 = (bf16[2,1,24576]{2,0,1:T(2,128)(2,1)S(1)}, bf16[2,1,24576]{2,0,1:T(2,128)(2,1)S(1)}, u32[]{:S(2)}, u32[]{:S(2)}) collective-permute-start(bf16[2,1,24576]{2,0,1:T(2,128)(2,1)S(1)} %collective-permute-done.3), channel_id=1, source_target_pairs={{0,30},{2,0},{4,2},{6,4},{8,6},{10,8},{12,10},{14,12},{16,14},{18,... | collective-permute-start | bytes 294920 | tf_op jit(solution)/shard_map/ppermute | solution.py:28
  150.5 4.5 %collective-permute-start.7 = (bf16[2,1,24576]{2,0,1:T(2,128)(2,1)S(1)}, bf16[2,1,24576]{2,0,1:T(2,128)(2,1)S(1)}, u32[]{:S(2)}, u32[]{:S(2)}) collective-permute-start(bf16[2,1,24576]{2,0,1:T(2,128)(2,1)S(1)} %collective-permute-done.5), channel_id=1, source_target_pairs={{0,30},{2,0},{4,2},{6,4},{8,6},{10,8},{12,10},{14,12},{16,14},{18,... | collective-permute-start | bytes 294920 | tf_op jit(solution)/shard_map/ppermute | solution.py:28
  157.4 4.5 %collective-permute-start.9 = (bf16[2,1,24576]{2,0,1:T(2,128)(2,1)S(1)}, bf16[2,1,24576]{2,0,1:T(2,128)(2,1)S(1)}, u32[]{:S(2)}, u32[]{:S(2)}) collective-permute-start(bf16[2,1,24576]{2,0,1:T(2,128)(2,1)S(1)} %collective-permute-done.7), channel_id=1, source_target_pairs={{0,30},{2,0},{4,2},{6,4},{8,6},{10,8},{12,10},{14,12},{16,14},{18,... | collective-permute-start | bytes 294920 | tf_op jit(solution)/shard_map/ppermute | solution.py:28
  164.1 4.6 %collective-permute-start.11 = (bf16[2,1,24576]{2,0,1:T(2,128)(2,1)S(1)}, bf16[2,1,24576]{2,0,1:T(2,128)(2,1)S(1)}, u32[]{:S(2)}, u32[]{:S(2)}) collective-permute-start(bf16[2,1,24576]{2,0,1:T(2,128)(2,1)S(1)} %collective-permute-done.9), channel_id=1, source_target_pairs={{0,30},{2,0},{4,2},{6,4},{8,6},{10,8},{12,10},{14,12},{16,14},{18,... | collective-permute-start | bytes 294920 | tf_op jit(solution)/shard_map/ppermute | solution.py:28
  171.0 4.6 %collective-permute-start.13 = (bf16[2,1,24576]{2,0,1:T(2,128)(2,1)S(1)}, bf16[2,1,24576]{2,0,1:T(2,128)(2,1)S(1)}, u32[]{:S(2)}, u32[]{:S(2)}) collective-permute-start(bf16[2,1,24576]{2,0,1:T(2,128)(2,1)S(1)} %collective-permute-done.11), channel_id=1, source_target_pairs={{0,30},{2,0},{4,2},{6,4},{8,6},{10,8},{12,10},{14,12},{16,14},{18,... | collective-permute-start | bytes 294920 | tf_op jit(solution)/shard_map/ppermute | solution.py:28
  179.6 3.4 %dynamic_update_slice.48 = bf16[2,16,24576]{2,1,0:T(8,128)(2,1)S(1)} dynamic-update-slice(bf16[2,16,24576]{2,1,0:T(8,128)(2,1)S(1)} %broadcast_in_dim.2, bf16[2,1,24576]{2,1,0:T(2,128)(2,1)S(1)} %copy.36, s32[]{:T(128)} %constant.115.clone.1, s32[]{:T(128)S(6)} %select_n.111, s32[]{:T(128)} %constant.115.clone.1) | dynamic-update-slice | bytes 196612 | tf_op jit(solution)/shard_map/dynamic_update_slice | solution.py:21
  183.2 3.4 %dynamic_update_slice.49 = bf16[2,16,24576]{2,1,0:T(8,128)(2,1)S(1)} dynamic-update-slice(bf16[2,16,24576]{2,1,0:T(8,128)(2,1)S(1)} %dynamic_update_slice.48, bf16[2,1,24576]{2,1,0:T(2,128)(2,1)S(1)} %copy.37, s32[]{:T(128)} %constant.115.clone.1, s32[]{:T(128)S(6)} %select_n.113, s32[]{:T(128)} %constant.115.clone.1) | dynamic-update-slice | bytes 196612 | tf_op jit(solution)/shard_map/dynamic_update_slice | solution.py:26
  186.7 3.4 %dynamic_update_slice.50 = bf16[2,16,24576]{2,1,0:T(8,128)(2,1)S(1)} dynamic-update-slice(bf16[2,16,24576]{2,1,0:T(8,128)(2,1)S(1)} %dynamic_update_slice.49, bf16[2,1,24576]{2,1,0:T(2,128)(2,1)S(1)} %copy.38, s32[]{:T(128)} %constant.115.clone.1, s32[]{:T(128)S(6)} %select_n.115, s32[]{:T(128)} %constant.115.clone.1) | dynamic-update-slice | bytes 196612 | tf_op jit(solution)/shard_map/dynamic_update_slice | solution.py:29
  190.2 3.4 %dynamic_update_slice.51 = bf16[2,16,24576]{2,1,0:T(8,128)(2,1)S(1)} dynamic-update-slice(bf16[2,16,24576]{2,1,0:T(8,128)(2,1)S(1)} %dynamic_update_slice.50, bf16[2,1,24576]{2,1,0:T(2,128)(2,1)S(1)} %copy.39, s32[]{:T(128)} %constant.115.clone.1, s32[]{:T(128)S(6)} %select_n.117, s32[]{:T(128)} %constant.115.clone.1) | dynamic-update-slice | bytes 196612 | tf_op jit(solution)/shard_map/dynamic_update_slice | solution.py:26
  193.7 3.4 %dynamic_update_slice.52 = bf16[2,16,24576]{2,1,0:T(8,128)(2,1)S(1)} dynamic-update-slice(bf16[2,16,24576]{2,1,0:T(8,128)(2,1)S(1)} %dynamic_update_slice.51, bf16[2,1,24576]{2,1,0:T(2,128)(2,1)S(1)} %copy.40, s32[]{:T(128)} %constant.115.clone.1, s32[]{:T(128)S(6)} %select_n.119, s32[]{:T(128)} %constant.115.clone.1) | dynamic-update-slice | bytes 196612 | tf_op jit(solution)/shard_map/dynamic_update_slice | solution.py:29
  197.3 3.4 %dynamic_update_slice.53 = bf16[2,16,24576]{2,1,0:T(8,128)(2,1)S(1)} dynamic-update-slice(bf16[2,16,24576]{2,1,0:T(8,128)(2,1)S(1)} %dynamic_update_slice.52, bf16[2,1,24576]{2,1,0:T(2,128)(2,1)S(1)} %copy.41, s32[]{:T(128)} %constant.115.clone.1, s32[]{:T(128)S(6)} %select_n.121, s32[]{:T(128)} %constant.115.clone.1) | dynamic-update-slice | bytes 196612 | tf_op jit(solution)/shard_map/dynamic_update_slice | solution.py:26
  204.3 3.4 %dynamic_update_slice.55 = bf16[2,16,24576]{2,1,0:T(8,128)(2,1)S(1)} dynamic-update-slice(bf16[2,16,24576]{2,1,0:T(8,128)(2,1)S(1)} %dynamic_update_slice.54, bf16[2,1,24576]{2,1,0:T(2,128)(2,1)S(1)} %copy.43, s32[]{:T(128)} %constant.115.clone.1, s32[]{:T(128)S(6)} %select_n.125, s32[]{:T(128)} %constant.115.clone.1) | dynamic-update-slice | bytes 196612 | tf_op jit(solution)/shard_map/dynamic_update_slice | solution.py:26
  207.9 3.4 %dynamic_update_slice.56 = bf16[2,16,24576]{2,1,0:T(8,128)(2,1)S(1)} dynamic-update-slice(bf16[2,16,24576]{2,1,0:T(8,128)(2,1)S(1)} %dynamic_update_slice.55, bf16[2,1,24576]{2,1,0:T(2,128)(2,1)S(1)} %copy.44, s32[]{:T(128)} %constant.115.clone.1, s32[]{:T(128)S(6)} %select_n.127, s32[]{:T(128)} %constant.115.clone.1) | dynamic-update-slice | bytes 196612 | tf_op jit(solution)/shard_map/dynamic_update_slice | solution.py:29
  211.4 3.4 %dynamic_update_slice.57 = bf16[2,16,24576]{2,1,0:T(8,128)(2,1)S(1)} dynamic-update-slice(bf16[2,16,24576]{2,1,0:T(8,128)(2,1)S(1)} %dynamic_update_slice.56, bf16[2,1,24576]{2,1,0:T(2,128)(2,1)S(1)} %copy.45, s32[]{:T(128)} %constant.115.clone.1, s32[]{:T(128)S(6)} %select_n.129, s32[]{:T(128)} %constant.115.clone.1) | dynamic-update-slice | bytes 196612 | tf_op jit(solution)/shard_map/dynamic_update_slice | solution.py:26
  214.9 3.4 %dynamic_update_slice.58 = bf16[2,16,24576]{2,1,0:T(8,128)(2,1)S(1)} dynamic-update-slice(bf16[2,16,24576]{2,1,0:T(8,128)(2,1)S(1)} %dynamic_update_slice.57, bf16[2,1,24576]{2,1,0:T(2,128)(2,1)S(1)} %copy.46, s32[]{:T(128)} %constant.115.clone.1, s32[]{:T(128)S(6)} %select_n.131, s32[]{:T(128)} %constant.115.clone.1) | dynamic-update-slice | bytes 196612 | tf_op jit(solution)/shard_map/dynamic_update_slice | solution.py:29
  218.5 3.4 %dynamic_update_slice.59 = bf16[2,16,24576]{2,1,0:T(8,128)(2,1)S(1)} dynamic-update-slice(bf16[2,16,24576]{2,1,0:T(8,128)(2,1)S(1)} %dynamic_update_slice.58, bf16[2,1,24576]{2,1,0:T(2,128)(2,1)S(1)} %copy.47, s32[]{:T(128)} %constant.115.clone.1, s32[]{:T(128)S(6)} %select_n.133, s32[]{:T(128)} %constant.115.clone.1) | dynamic-update-slice | bytes 196612 | tf_op jit(solution)/shard_map/dynamic_update_slice | solution.py:26
  222.0 3.4 %dynamic_update_slice.60 = bf16[2,16,24576]{2,1,0:T(8,128)(2,1)S(1)} dynamic-update-slice(bf16[2,16,24576]{2,1,0:T(8,128)(2,1)S(1)} %dynamic_update_slice.59, bf16[2,1,24576]{2,1,0:T(2,128)(2,1)S(1)} %copy.48, s32[]{:T(128)} %constant.115.clone.1, s32[]{:T(128)S(6)} %select_n.135, s32[]{:T(128)} %constant.115.clone.1) | dynamic-update-slice | bytes 196612 | tf_op jit(solution)/shard_map/dynamic_update_slice | solution.py:29
  225.5 3.4 %dynamic_update_slice.61 = bf16[2,16,24576]{2,1,0:T(8,128)(2,1)S(1)} dynamic-update-slice(bf16[2,16,24576]{2,1,0:T(8,128)(2,1)S(1)} %dynamic_update_slice.60, bf16[2,1,24576]{2,1,0:T(2,128)(2,1)S(1)} %copy.49, s32[]{:T(128)} %constant.115.clone.1, s32[]{:T(128)S(6)} %select_n.137, s32[]{:T(128)} %constant.115.clone.1) | dynamic-update-slice | bytes 196612 | tf_op jit(solution)/shard_map/dynamic_update_slice | solution.py:26
  229.1 3.4 %dynamic_update_slice.62 = bf16[2,16,24576]{2,1,0:T(8,128)(2,1)S(1)} dynamic-update-slice(bf16[2,16,24576]{2,1,0:T(8,128)(2,1)S(1)} %dynamic_update_slice.61, bf16[2,1,24576]{2,1,0:T(2,128)(2,1)S(1)} %copy.50, s32[]{:T(128)} %constant.115.clone.1, s32[]{:T(128)S(6)} %select_n.139, s32[]{:T(128)} %constant.115.clone.1) | dynamic-update-slice | bytes 196612 | tf_op jit(solution)/shard_map/dynamic_update_slice | solution.py:29
  (65 shorter events, 34.2 us)
Async XLA Ops:
  0.6 43.7 %copy-start = (bf16[1,2,16,24576]{3,2,1,0:T(8,128)(2,1)S(1)}, bf16[1,2,16,24576]{3,2,1,0:T(8,128)(2,1)}, u32[]{:S(2)}) copy-start(bf16[1,2,16,24576]{3,2,1,0:T(8,128)(2,1)} %param.4) | copy-start | bytes 4718596
  87.5 1.4 copy-start.5
  87.5 1.6 copy-start.3
  87.5 1.6 copy-start.4
  89.0 90.6 %copy-start.2 = (bf16[2,1,24576]{2,0,1:T(2,128)(2,1)}, bf16[2,1,24576]{2,0,1:T(2,128)(2,1)S(1)}, u32[]{:S(2)}) copy-start(bf16[2,1,24576]{2,0,1:T(2,128)(2,1)S(1)} %fusion.2) | copy-start | bytes 294916
  130.1 6.9 %collective-permute-start = (bf16[2,1,24576]{2,0,1:T(2,128)(2,1)S(1)}, bf16[2,1,24576]{2,0,1:T(2,128)(2,1)S(1)}, u32[]{:S(2)}, u32[]{:S(2)}) collective-permute-start(bf16[2,1,24576]{2,0,1:T(2,128)(2,1)S(1)} %divide_convert_fusion.1), channel_id=1, source_target_pairs={{0,2},{2,4},{4,6},{6,8},{8,10},{10,12},{12,14},{14,16},{16,18},{18... | collective-permute-start | bytes 294920 | tf_op jit(solution)/shard_map/ppermute | solution.py:25
  130.2 6.8 %collective-permute-start.1 = (bf16[2,1,24576]{2,0,1:T(2,128)(2,1)S(1)}, bf16[2,1,24576]{2,0,1:T(2,128)(2,1)S(1)}, u32[]{:S(2)}, u32[]{:S(2)}) collective-permute-start(bf16[2,1,24576]{2,0,1:T(2,128)(2,1)S(1)} %divide_convert_fusion.1), channel_id=1, source_target_pairs={{0,30},{2,0},{4,2},{6,4},{8,6},{10,8},{12,10},{14,12},{16,14},{18,... | collective-permute-start | bytes 294920 | tf_op jit(solution)/shard_map/ppermute | solution.py:28
  137.0 6.7 %collective-permute-start.2 = (bf16[2,1,24576]{2,0,1:T(2,128)(2,1)S(1)}, bf16[2,1,24576]{2,0,1:T(2,128)(2,1)S(1)}, u32[]{:S(2)}, u32[]{:S(2)}) collective-permute-start(bf16[2,1,24576]{2,0,1:T(2,128)(2,1)S(1)} %collective-permute-done), channel_id=1, source_target_pairs={{0,2},{2,4},{4,6},{6,8},{8,10},{10,12},{12,14},{14,16},{16,18},{18... | collective-permute-start | bytes 294920 | tf_op jit(solution)/shard_map/ppermute | solution.py:25
  137.0 6.7 %collective-permute-start.3 = (bf16[2,1,24576]{2,0,1:T(2,128)(2,1)S(1)}, bf16[2,1,24576]{2,0,1:T(2,128)(2,1)S(1)}, u32[]{:S(2)}, u32[]{:S(2)}) collective-permute-start(bf16[2,1,24576]{2,0,1:T(2,128)(2,1)S(1)} %collective-permute-done.1), channel_id=1, source_target_pairs={{0,30},{2,0},{4,2},{6,4},{8,6},{10,8},{12,10},{14,12},{16,14},{18,... | collective-permute-start | bytes 294920 | tf_op jit(solution)/shard_map/ppermute | solution.py:28
  143.8 6.7 %collective-permute-start.4 = (bf16[2,1,24576]{2,0,1:T(2,128)(2,1)S(1)}, bf16[2,1,24576]{2,0,1:T(2,128)(2,1)S(1)}, u32[]{:S(2)}, u32[]{:S(2)}) collective-permute-start(bf16[2,1,24576]{2,0,1:T(2,128)(2,1)S(1)} %collective-permute-done.2), channel_id=1, source_target_pairs={{0,2},{2,4},{4,6},{6,8},{8,10},{10,12},{12,14},{14,16},{16,18},{18... | collective-permute-start | bytes 294920 | tf_op jit(solution)/shard_map/ppermute | solution.py:25
  143.8 6.7 %collective-permute-start.5 = (bf16[2,1,24576]{2,0,1:T(2,128)(2,1)S(1)}, bf16[2,1,24576]{2,0,1:T(2,128)(2,1)S(1)}, u32[]{:S(2)}, u32[]{:S(2)}) collective-permute-start(bf16[2,1,24576]{2,0,1:T(2,128)(2,1)S(1)} %collective-permute-done.3), channel_id=1, source_target_pairs={{0,30},{2,0},{4,2},{6,4},{8,6},{10,8},{12,10},{14,12},{16,14},{18,... | collective-permute-start | bytes 294920 | tf_op jit(solution)/shard_map/ppermute | solution.py:28
  150.5 6.8 %collective-permute-start.6 = (bf16[2,1,24576]{2,0,1:T(2,128)(2,1)S(1)}, bf16[2,1,24576]{2,0,1:T(2,128)(2,1)S(1)}, u32[]{:S(2)}, u32[]{:S(2)}) collective-permute-start(bf16[2,1,24576]{2,0,1:T(2,128)(2,1)S(1)} %collective-permute-done.4), channel_id=1, source_target_pairs={{0,2},{2,4},{4,6},{6,8},{8,10},{10,12},{12,14},{14,16},{16,18},{18... | collective-permute-start | bytes 294920 | tf_op jit(solution)/shard_map/ppermute | solution.py:25
  150.5 6.8 %collective-permute-start.7 = (bf16[2,1,24576]{2,0,1:T(2,128)(2,1)S(1)}, bf16[2,1,24576]{2,0,1:T(2,128)(2,1)S(1)}, u32[]{:S(2)}, u32[]{:S(2)}) collective-permute-start(bf16[2,1,24576]{2,0,1:T(2,128)(2,1)S(1)} %collective-permute-done.5), channel_id=1, source_target_pairs={{0,30},{2,0},{4,2},{6,4},{8,6},{10,8},{12,10},{14,12},{16,14},{18,... | collective-permute-start | bytes 294920 | tf_op jit(solution)/shard_map/ppermute | solution.py:28
  157.4 6.7 %collective-permute-start.8 = (bf16[2,1,24576]{2,0,1:T(2,128)(2,1)S(1)}, bf16[2,1,24576]{2,0,1:T(2,128)(2,1)S(1)}, u32[]{:S(2)}, u32[]{:S(2)}) collective-permute-start(bf16[2,1,24576]{2,0,1:T(2,128)(2,1)S(1)} %collective-permute-done.6), channel_id=1, source_target_pairs={{0,2},{2,4},{4,6},{6,8},{8,10},{10,12},{12,14},{14,16},{16,18},{18... | collective-permute-start | bytes 294920 | tf_op jit(solution)/shard_map/ppermute | solution.py:25
  157.4 6.8 %collective-permute-start.9 = (bf16[2,1,24576]{2,0,1:T(2,128)(2,1)S(1)}, bf16[2,1,24576]{2,0,1:T(2,128)(2,1)S(1)}, u32[]{:S(2)}, u32[]{:S(2)}) collective-permute-start(bf16[2,1,24576]{2,0,1:T(2,128)(2,1)S(1)} %collective-permute-done.7), channel_id=1, source_target_pairs={{0,30},{2,0},{4,2},{6,4},{8,6},{10,8},{12,10},{14,12},{16,14},{18,... | collective-permute-start | bytes 294920 | tf_op jit(solution)/shard_map/ppermute | solution.py:28
  164.1 6.7 %collective-permute-start.10 = (bf16[2,1,24576]{2,0,1:T(2,128)(2,1)S(1)}, bf16[2,1,24576]{2,0,1:T(2,128)(2,1)S(1)}, u32[]{:S(2)}, u32[]{:S(2)}) collective-permute-start(bf16[2,1,24576]{2,0,1:T(2,128)(2,1)S(1)} %collective-permute-done.8), channel_id=1, source_target_pairs={{0,2},{2,4},{4,6},{6,8},{8,10},{10,12},{12,14},{14,16},{16,18},{18... | collective-permute-start | bytes 294920 | tf_op jit(solution)/shard_map/ppermute | solution.py:25
  164.1 6.8 %collective-permute-start.11 = (bf16[2,1,24576]{2,0,1:T(2,128)(2,1)S(1)}, bf16[2,1,24576]{2,0,1:T(2,128)(2,1)S(1)}, u32[]{:S(2)}, u32[]{:S(2)}) collective-permute-start(bf16[2,1,24576]{2,0,1:T(2,128)(2,1)S(1)} %collective-permute-done.9), channel_id=1, source_target_pairs={{0,30},{2,0},{4,2},{6,4},{8,6},{10,8},{12,10},{14,12},{16,14},{18,... | collective-permute-start | bytes 294920 | tf_op jit(solution)/shard_map/ppermute | solution.py:28
  170.8 6.7 %collective-permute-start.12 = (bf16[2,1,24576]{2,0,1:T(2,128)(2,1)S(1)}, bf16[2,1,24576]{2,0,1:T(2,128)(2,1)S(1)}, u32[]{:S(2)}, u32[]{:S(2)}) collective-permute-start(bf16[2,1,24576]{2,0,1:T(2,128)(2,1)S(1)} %collective-permute-done.10), channel_id=1, source_target_pairs={{0,2},{2,4},{4,6},{6,8},{8,10},{10,12},{12,14},{14,16},{16,18},{18... | collective-permute-start | bytes 294920 | tf_op jit(solution)/shard_map/ppermute | solution.py:25
  171.0 57.9 %collective-permute-start.13 = (bf16[2,1,24576]{2,0,1:T(2,128)(2,1)S(1)}, bf16[2,1,24576]{2,0,1:T(2,128)(2,1)S(1)}, u32[]{:S(2)}, u32[]{:S(2)}) collective-permute-start(bf16[2,1,24576]{2,0,1:T(2,128)(2,1)S(1)} %collective-permute-done.11), channel_id=1, source_target_pairs={{0,30},{2,0},{4,2},{6,4},{8,6},{10,8},{12,10},{14,12},{16,14},{18,... | collective-permute-start | bytes 294920 | tf_op jit(solution)/shard_map/ppermute | solution.py:28
  177.6 54.8 %collective-permute-start.14 = (bf16[2,1,24576]{2,0,1:T(2,128)(2,1)S(1)}, bf16[2,1,24576]{2,0,1:T(2,128)(2,1)S(1)}, u32[]{:S(2)}, u32[]{:S(2)}) collective-permute-start(bf16[2,1,24576]{2,0,1:T(2,128)(2,1)S(1)} %collective-permute-done.12), channel_id=1, source_target_pairs={{0,2},{2,4},{4,6},{6,8},{8,10},{10,12},{12,14},{14,16},{16,18},{18... | collective-permute-start | bytes 294920 | tf_op jit(solution)/shard_map/ppermute | solution.py:25
  236.0 1.1 copy-start.1
